TPU v7x, 32 devices: a whole 2x2x4 slice. The times are simulated.
32 devices in a mesh: grp: 4 (over z), ctx: 2 (over y), wid: 4 (over x, core).
Axes of the slice: x: 2, y: 2, z: 4, core: 2. Of those that a mesh axis runs over, the one named last changes fastest.
Arguments:
- query: bfloat16 [256, 64, 128], P(None, 'wid'), may hold values from -64 to 64
- keys: bfloat16 [4, 512, 8, 128], P(None, ('grp', 'ctx'), 'wid'), may hold values from -64 to 64
- values: bfloat16 [4, 512, 8, 128], P(None, ('grp', 'ctx'), 'wid'), may hold values from -6 to 6
- lengths: int32 [4, 8], replicated, may hold values from 32 to 64
- query_pos: int32 [256], replicated, may hold values from 128 to 511
- resid: bfloat16 [256, 5120], P('wid', ('grp', 'ctx')), may hold values from -1.1953125 to 1.1953125
- out_weight: bfloat16 [8192, 5120], P('wid', ('grp', 'ctx')), may hold values from -0.0625 to 0.0625
- enc_weight: bfloat16 [5120, 24576], P('wid', ('grp', 'ctx')), may hold values from -0.078125 to 0.078125
- enc_bias: float32 [24576], P(('grp', 'ctx')), may hold values from -3 to 3
- dec_weight: bfloat16 [24576, 5120], P(('grp', 'ctx'), 'wid'), may hold values from -0.078125 to 0.078125
- dec_bias: float32 [5120], P('wid'), may hold values from -3 to 3
Outputs:
- layer_out: bfloat16 [256, 5120], P('wid', ('grp', 'ctx'))
- enc_grad: bfloat16 [5120, 24576], P('wid', ('grp', 'ctx'))
- enc_bias_grad: float32 [24576], P(('grp', 'ctx'))
- dec_grad: bfloat16 [24576, 5120], P(('grp', 'ctx'), 'wid')
- dec_bias_grad: float32 [5120], P('wid')
Inputs may be any that keep to these rules, and one draw needn't show every extreme that they name: `lengths`: live slots of a shard are its first ones.
All inputs are finite; a program needn't handle non-finite values.
Results may differ from a plain program's by a relative error of at most 0.024.
Values may be sent and summed in bfloat16 or wider, within the bound.
A program may use at most 128 MiB of HBM per device.

v0:
```python
import jax
import jax.numpy as jnp
from jax import lax
from jax.sharding import PartitionSpec as P

HD = 128


def body(
    query,
    keys,
    values,
    lengths,
    query_pos,
    resid,
    out_weight,
    enc_weight,
    enc_bias,
    dec_weight,
    dec_bias,
):
    seq_count, slot_count, kv_local, head_dim = keys.shape
    row_count = query.shape[0]
    heads_local = query.shape[1]
    group_size = heads_local // kv_local
    rows_each = row_count // seq_count
    shard_pos = lax.axis_index(("grp", "ctx"))
    shard_ids = jnp.arange(lengths.shape[1], dtype=jnp.int32)
    offset = jnp.sum(jnp.where(shard_ids[None, :] < shard_pos, lengths, 0), axis=1)
    live_count = jnp.sum(jnp.where(shard_ids[None, :] == shard_pos, lengths, 0), axis=1)
    slot_ids = jnp.arange(slot_count, dtype=jnp.int32)
    key_pos = offset[:, None] + slot_ids[None, :]
    live_slot = slot_ids[None, :] < live_count[:, None]
    row_position = query_pos.reshape(seq_count, rows_each)
    visible = live_slot[:, None, :] & (key_pos[:, None, :] <= row_position[:, :, None])
    visible_mask = visible[:, :, None, None, :]
    q_view = query.reshape(seq_count, rows_each, kv_local, group_size, head_dim)
    scores = jnp.einsum(
        "srkgd,sjkd->srkgj", q_view, keys, preferred_element_type=jnp.float32
    ) * HD ** (-0.5)
    local_peak = jnp.max(jnp.where(visible_mask, scores, -1e30), axis=-1)
    peak = lax.pmax(local_peak, ("grp", "ctx"))
    weights = jnp.where(visible_mask, jnp.exp(scores - peak[..., None]), 0.0)
    weight_sum = jnp.sum(weights, axis=-1)
    weights_low = weights.astype(jnp.bfloat16)
    weighted = jnp.einsum(
        "srkgj,sjkd->srkgd", weights_low, values, preferred_element_type=jnp.float32
    )
    weight_sum, weighted = (weight_sum, weighted)
    weight_sum, weighted = lax.psum((weight_sum, weighted), ("grp", "ctx"))
    attention = (weighted / weight_sum[..., None]).astype(jnp.bfloat16)
    attention = attention.reshape(row_count, heads_local * head_dim)
    projected = jnp.dot(attention, out_weight, preferred_element_type=jnp.float32)
    mixed = lax.psum_scatter(
        projected.astype(jnp.bfloat16), "wid", scatter_dimension=0, tiled=True
    ).astype(jnp.float32)
    layer_out = (mixed + resid.astype(jnp.float32)).astype(jnp.bfloat16)
    wide_rows = lax.all_gather(layer_out, ("grp", "ctx"), axis=1, tiled=True)
    block = lax.all_to_all(wide_rows, "wid", split_axis=1, concat_axis=0, tiled=True)
    enc_part = jnp.dot(block, enc_weight, preferred_element_type=jnp.float32)
    preact = lax.psum(enc_part.astype(jnp.bfloat16), "wid").astype(jnp.float32) + enc_bias
    latents = (jax.nn.softplus(4.0 * preact) * 0.25).astype(jnp.bfloat16)
    row_scale = row_count ** (-0.5)
    recon = lax.psum_scatter(
        jnp.dot(latents, dec_weight, preferred_element_type=jnp.float32),
        ("grp", "ctx"),
        scatter_dimension=0,
        tiled=True,
    )
    piece_len = recon.shape[0]
    target = lax.dynamic_slice_in_dim(block, shard_pos * piece_len, piece_len, 0).astype(
        jnp.float32
    )
    scaled_error = ((recon + dec_bias - target) * row_scale).astype(jnp.bfloat16)
    error_all = lax.all_gather(scaled_error, ("grp", "ctx"), axis=0, tiled=True)
    dec_bias_grad = jnp.sum(error_all, axis=0, dtype=jnp.float32)
    latent_part = lax.dot_general(
        error_all, dec_weight, (((1,), (1,)), ((), ())), preferred_element_type=jnp.float32
    )
    dec_grad = lax.dot_general(
        latents, error_all, (((0,), (0,)), ((), ())), preferred_element_type=jnp.float32
    )
    latent_grad = lax.psum(latent_part.astype(jnp.bfloat16), "wid").astype(jnp.float32)
    preact_grad = (latent_grad * jax.nn.sigmoid(4.0 * preact)).astype(jnp.bfloat16)
    enc_grad = lax.dot_general(
        block, preact_grad, (((0,), (0,)), ((), ())), preferred_element_type=jnp.float32
    ).astype(jnp.bfloat16)
    enc_bias_grad = jnp.sum(preact_grad, axis=0, dtype=jnp.float32)
    return (layer_out, enc_grad, enc_bias_grad, dec_grad.astype(jnp.bfloat16), dec_bias_grad)


def solution(mesh):
    placed = (
        P(None, "wid", None),
        P(None, ("grp", "ctx"), "wid", None),
        P(None, ("grp", "ctx"), "wid", None),
        P(),
        P(),
        P("wid", ("grp", "ctx")),
        P("wid", ("grp", "ctx")),
        P("wid", ("grp", "ctx")),
        P(("grp", "ctx")),
        P(("grp", "ctx"), "wid"),
        P("wid"),
    )
    return jax.shard_map(
        body,
        mesh=mesh,
        in_specs=placed,
        out_specs=(
            P("wid", ("grp", "ctx")),
            P("wid", ("grp", "ctx")),
            P(("grp", "ctx")),
            P(("grp", "ctx"), "wid"),
            P("wid"),
        ),
        check_vma=False,
    )
```

profile of v0, /device:TPU:0, one launch (start us, length us, event | category | flops | bytes accessed | tf_op | source)
XLA Modules:
  0.0 456.0 jit_solution(1669517848478432027)
XLA Ops:
  7.2 0.0 copy-start
  7.2 0.0 all-reduce.4.cloned.1.call-start
  7.2 0.9 le.20
  8.1 0.8 select_reduce_fusion.1
  9.0 0.1 iota_add_fusion
  9.0 0.1 iota_compare_fusion
  9.1 0.1 compare_and_fusion
  9.3 3.8 fusion.2
  13.0 39.0 %pmax.7 = f32[4,64,2,8]{1,3,2,0:T(8,128)S(1)} all-reduce(f32[4,64,2,8]{1,3,2,0:T(8,128)S(1)} %get-tuple-element.11), channel_id=1, replica_groups=mesh['grp'=4,'ctx'=2,'wid'=4] {'grp','ctx'}, use_global_device_ids=true, to_apply=%region_3.4 | all-reduce | flops 4096 | bytes 32768 | tf_op jit(solution)/shard_map/pmax | solution.py:42
  52.0 3.2 fusion.5
  55.3 2.4 copy.29
  57.7 3.0 convolution_bitcast_fusion
  60.6 0.0 all-reduce.4.cloned.1.call-update
  60.7 0.0 reduce-scatter.3.cloned.1.call-start
  60.7 34.2 %psum.29 = f32[4,64,2,8]{1,3,2,0:T(8,128)S(1)} all-reduce(f32[4,64,2,8]{1,3,2,0:T(8,128)S(1)} %get-tuple-element.9), channel_id=1, replica_groups=mesh['grp'=4,'ctx'=2,'wid'=4] {'grp','ctx'}, use_global_device_ids=true, to_apply=%region_6.7 | all-reduce | flops 4096 | bytes 32768 | tf_op jit(solution)/shard_map/psum | solution.py:50
  94.9 0.1 copy.31
  95.0 65.7 %all-reduce.4.cloned.1.call-done = f32[4,64,2,8,128]{4,3,1,2,0:T(8,128)} async-done(((f32[4,64,2,8,128]{4,3,1,2,0:T(8,128)}), f32[4,64,2,8,128]{4,3,1,2,0:T(8,128)}) %all-reduce.4.cloned.1.call-update) | async-done | bytes 2097168 | tf_op jit(solution)/shard_map/psum | solution.py:50
  160.8 1.9 divide_convert_fusion
  162.7 1.2 copy.32
  163.9 2.3 reshape.71
  166.2 2.9 convolution_convert_fusion.4
  169.1 0.0 reduce-scatter.3.cloned.1.call-update
  169.1 0.0 all-reduce.6.cloned.1.call-start
  169.2 19.8 %reduce-scatter.3.cloned.1.call-done = bf16[64,640]{1,0:T(8,128)(2,1)} async-done(((bf16[256,640]{1,0:T(8,128)(2,1)}), bf16[64,640]{1,0:T(8,128)(2,1)}) %reduce-scatter.3.cloned.1.call-update) | async-done | bytes 81936 | tf_op jit(solution)/shard_map/reduce_scatter | solution.py:54
  189.0 0.9 add_convert_fusion
  189.9 0.0 copy-start.2
  189.9 32.1 %all_gather.6 = bf16[64,5120]{1,0:T(8,128)(2,1)S(1)} all-gather(bf16[64,640]{1,0:T(8,128)(2,1)S(1)} %add_convert_fusion), channel_id=1, replica_groups=mesh['grp'=4,'ctx'=2,'wid'=4] {'grp','ctx'}, dimensions={1}, use_global_device_ids=true | all-gather | bytes 737280 | tf_op jit(solution)/shard_map/all_gather | solution.py:58
  222.1 12.6 %all_to_all.19 = bf16[64,4,1280]{2,0,1:T(8,128)(2,1)S(1)} all-to-all(bf16[64,4,1280]{2,0,1:T(8,128)(2,1)S(1)} %bitcast.41), channel_id=1, replica_groups=mesh['grp'=4,'ctx'=2,'wid'=4] {'wid'}, dimensions={1} | all-to-all | bytes 1310720 | tf_op jit(solution)/shard_map/all_to_all | solution.py:59
  234.7 6.6 %convolution_convert_fusion.3 = bf16[256,3072]{1,0:T(8,128)(2,1)} fusion(bf16[256,1280]{1,0:T(8,128)(2,1)S(1)} %bitcast.38, bf16[1280,3072]{1,0:T(8,128)(2,1)} %param.18), kind=kOutput, calls=%fused_computation.4 | convolution fusion | flops 2014052352 | bytes 10092544 | tf_op jit(solution)/shard_map/dot_general | solution.py:60
  241.3 0.0 all-reduce.6.cloned.1.call-update
  241.4 0.0 copy-start.6
  241.4 0.0 reduce-scatter.5.cloned.1.call-start
  241.4 42.7 %all-reduce.6.cloned.1.call-done = bf16[256,3072]{1,0:T(8,128)(2,1)} async-done(((bf16[256,3072]{1,0:T(8,128)(2,1)}), bf16[256,3072]{1,0:T(8,128)(2,1)}) %all-reduce.6.cloned.1.call-update) | async-done | bytes 1572880 | tf_op jit(solution)/shard_map/psum | solution.py:61
  284.1 8.8 %fusion.12 = f32[256,1280]{1,0:T(8,128)} fusion(bf16[3072,1280]{1,0:T(8,128)(2,1)} %param.20, bf16[256,3072]{1,0:T(8,128)(2,1)} %all-reduce.6.cloned.1.call-done, f32[3072]{0:T(1024)S(1)} %copy-done.5), kind=kOutput, calls=%fused_computation.35 | convolution fusion | flops 2021916672 | bytes 10760192 | tf_op jit(solution)/shard_map/dot_general | solution.py:65
  292.9 0.0 reduce-scatter.5.cloned.1.call-update
  293.0 0.0 all-reduce.8.cloned.1.call-start
  293.0 65.3 %reduce-scatter.5.cloned.1.call-done = f32[32,1280]{1,0:T(8,128)} async-done(((f32[256,1280]{1,0:T(8,128)}), f32[32,1280]{1,0:T(8,128)}) %reduce-scatter.5.cloned.1.call-update) | async-done | bytes 163856 | tf_op jit(solution)/shard_map/reduce_scatter | solution.py:64
  358.3 0.0 copy-done.6
  358.3 0.9 multiply_convert_fusion.1
  359.2 32.1 %all_gather.7 = bf16[256,1280]{1,0:T(8,128)(2,1)S(1)} all-gather(bf16[32,1280]{1,0:T(8,128)(2,1)S(1)} %multiply_convert_fusion.1), channel_id=1, replica_groups=mesh['grp'=4,'ctx'=2,'wid'=4] {'grp','ctx'}, dimensions={0}, use_global_device_ids=true | all-gather | bytes 737280 | tf_op jit(solution)/shard_map/all_gather | solution.py:75
  391.4 0.8 copy-done.1
  392.2 6.6 %convolution_convert_fusion.2 = bf16[256,3072]{1,0:T(8,128)(2,1)} fusion(bf16[256,1280]{1,0:T(8,128)(2,1)S(1)} %all_gather.7, bf16[3072,1280]{1,0:T(8,128)(2,1)} %param.20), kind=kOutput, calls=%fused_computation.3 | convolution fusion | flops 2014052352 | bytes 10092544 | tf_op jit(solution)/shard_map/dot_general | solution.py:77
  398.8 0.0 all-reduce.8.cloned.1.call-update
  398.8 1.8 convert_reduce_fusion.1
  400.6 9.0 %convolution_convert_fusion = bf16[3072,1280]{1,0:T(8,128)(2,1)} fusion(bf16[256,1280]{1,0:T(8,128)(2,1)} %copy-done.1, bf16[256,3072]{1,0:T(8,128)(2,1)} %all-reduce.6.cloned.1.call-done, f32[3072]{0:T(1024)S(1)} %copy-done.5), kind=kOutput, calls=%fused_computation | convolution fusion | flops 2025848832 | bytes 10104832 | tf_op jit(solution)/shard_map/dot_general | solution.py:80
  409.6 30.8 %all-reduce.8.cloned.1.call-done = bf16[256,3072]{1,0:T(8,128)(2,1)} async-done(((bf16[256,3072]{1,0:T(8,128)(2,1)}), bf16[256,3072]{1,0:T(8,128)(2,1)}) %all-reduce.8.cloned.1.call-update) | async-done | bytes 1572880 | tf_op jit(solution)/shard_map/psum | solution.py:83
  440.4 3.6 convert_reduce_fusion
  444.0 5.5 %convolution_convert_fusion.1 = bf16[1280,3072]{1,0:T(8,128)(2,1)} fusion(bf16[256,1280]{1,0:T(8,128)(2,1)S(1)} %bitcast.40, bf16[256,3072]{1,0:T(8,128)(2,1)S(1)} %get-tuple-element.8), kind=kOutput, calls=%fused_computation.1 | convolution fusion | flops 2017198080 | bytes 10092544 | tf_op jit(solution)/shard_map/dot_general | solution.py:85
  (11 shorter events, 0.1 us)
Async XLA Ops:
  7.2 159.0 %copy-start = (bf16[2048,640]{1,0:T(8,128)(2,1)S(1)}, bf16[2048,640]{1,0:T(8,128)(2,1)}, u32[]{:S(2)}) copy-start(bf16[2048,640]{1,0:T(8,128)(2,1)} %param.17) | copy-start | bytes 7864324
  7.2 153.6 %all-reduce.4.cloned.1.call-start = ((), (), s32[]{:S(2)}) async-start(), calls=%async_computation.3 | async-start | bytes 4194304 | tf_op jit(solution)/shard_map/psum | solution.py:50
  13.0 44.6 %copy-start.3 = (bf16[4,64,2,128]{3,2,1,0:T(2,128)(2,1)S(1)}, bf16[4,64,2,128]{3,2,1,0:T(2,128)(2,1)}, u32[]{:S(2)}) copy-start(bf16[4,64,2,128]{3,2,1,0:T(2,128)(2,1)} %param.13) | copy-start | bytes 393220
  60.7 128.4 %reduce-scatter.3.cloned.1.call-start = ((), (), s32[]{:S(2)}) async-start(), calls=%async_computation.4 | async-start | bytes 409600 | tf_op jit(solution)/shard_map/reduce_scatter | solution.py:54
  163.9 25.1 %copy-start.4 = (bf16[64,640]{1,0:T(8,128)(2,1)S(1)}, bf16[64,640]{1,0:T(8,128)(2,1)}, u32[]{:S(2)}) copy-start(bf16[64,640]{1,0:T(8,128)(2,1)} %param.16) | copy-start | bytes 245764
  169.1 114.9 %all-reduce.6.cloned.1.call-start = ((), (), s32[]{:S(2)}) async-start(), calls=%async_computation.5 | async-start | bytes 3145728 | tf_op jit(solution)/shard_map/psum | solution.py:61
  189.9 51.4 %copy-start.2 = (bf16[64,640]{1,0:T(8,128)(2,1)}, bf16[64,640]{1,0:T(8,128)(2,1)S(1)}, u32[]{:S(2)}) copy-start(bf16[64,640]{1,0:T(8,128)(2,1)S(1)} %add_convert_fusion) | copy-start | bytes 245764
  234.7 49.3 %copy-start.5 = (f32[3072]{0:T(1024)S(1)}, f32[3072]{0:T(1024)}, u32[]{:S(2)}) copy-start(f32[3072]{0:T(1024)} %param.19) | copy-start | bytes 36868
  241.4 116.9 %copy-start.6 = (f32[1280]{0:T(1024)S(1)}, f32[1280]{0:T(1024)}, u32[]{:S(2)}) copy-start(f32[1280]{0:T(1024)} %param.21) | copy-start | bytes 15364
  241.4 116.9 %reduce-scatter.5.cloned.1.call-start = ((), (), s32[]{:S(2)}) async-start(), calls=%async_computation.6 | async-start | bytes 1474560 | tf_op jit(solution)/shard_map/reduce_scatter | solution.py:64
  293.0 147.5 %all-reduce.8.cloned.1.call-start = ((), (), s32[]{:S(2)}) async-start(), calls=%async_computation.7 | async-start | bytes 3145728 | tf_op jit(solution)/shard_map/psum | solution.py:83
  391.4 0.8 copy-start.1
Sparse Core Ops, SparseCore 0:
  60.8 99.9 all-reduce.3
  169.3 19.6 reduce-scatter.2
  241.5 42.5 all-reduce.5
  293.1 65.1 reduce-scatter.4
  398.9 41.4 all-reduce.7
where the time goes:
time: 457 us; the launch traced here: 456 us
  waiting for transfers between devices  224 us (49%)
  blocking collectives  150 us (33%)
  matrix products  46.2 us (10%)
  between operations  13.9 us (3%)
  other arithmetic  13.5 us (3%)
  local copies, waits for them, and re-layouts  7.82 us (2%)
    psum x1, waiting for transfers between devices, body(): weight_sum, weighted = lax.psum((weight_sum, weighted), ('grp', 'ctx'))  65.7 us
    reduce_scatter x1, waiting for transfers between devices, body(): lax.psum_scatter(jnp.dot(latents, dec_weight, preferred_element_type=jnp....  65.3 us
    psum x1, waiting for transfers between devices, body(): lax.psum(enc_part.astype(jnp.bfloat16), 'wid').astype(jnp.float32)  42.7 us
    pmax x1, blocking collectives, body(): peak = lax.pmax(local_peak, ('grp', 'ctx'))  39 us
    psum x1, blocking collectives, body(): weight_sum, weighted = lax.psum((weight_sum, weighted), ('grp', 'ctx'))  34.2 us
    all_gather x1, blocking collectives, body(): wide_rows = lax.all_gather(layer_out, ('grp', 'ctx'), axis=1, tiled=True)  32.1 us
    all_gather x1, blocking collectives, body(): error_all = lax.all_gather(scaled_error, ('grp', 'ctx'), axis=0, tiled=True)  32.1 us
    psum x1, waiting for transfers between devices, body(): lax.psum(latent_part.astype(jnp.bfloat16), 'wid').astype(jnp.float32)  30.8 us
  transfers between devices with their start and end apart: 5, of which 5 were waited for; matrix products, arithmetic and copies ran while one was open for 2% of the time, Pallas kernels for 0%

commit v1 on v0

--- a/solution.py
+++ b/solution.py
@@ -55,7 +55,7 @@
         projected.astype(jnp.bfloat16), "wid", scatter_dimension=0, tiled=True
     ).astype(jnp.float32)
     layer_out = (mixed + resid.astype(jnp.float32)).astype(jnp.bfloat16)
-    wide_rows = lax.all_gather(layer_out, ("grp", "ctx"), axis=1, tiled=True)
+    wide_rows = jnp.concatenate(lax.all_gather(layer_out, ("grp", "ctx")), axis=1)
     block = lax.all_to_all(wide_rows, "wid", split_axis=1, concat_axis=0, tiled=True)
     enc_part = jnp.dot(block, enc_weight, preferred_element_type=jnp.float32)
     preact = lax.psum(enc_part.astype(jnp.bfloat16), "wid").astype(jnp.float32) + enc_bias

time: 457 us -> 460 us (level)
  no operation moved by 1% of the time
where the time goes in v1:
time: 460 us; the launch traced here: 459 us
  waiting for transfers between devices  225 us (49%)
  blocking collectives  150 us (33%)
  matrix products  46.2 us (10%)
  between operations  13.9 us (3%)
  other arithmetic  13.5 us (3%)
  local copies, waits for them, and re-layouts  10.6 us (2%)
    psum x1, waiting for transfers between devices, body(): weight_sum, weighted = lax.psum((weight_sum, weighted), ('grp', 'ctx'))  65.7 us
    reduce_scatter x1, waiting for transfers between devices, body(): lax.psum_scatter(jnp.dot(latents, dec_weight, preferred_element_type=jnp....  65.3 us
    psum x1, waiting for transfers between devices, body(): lax.psum(enc_part.astype(jnp.bfloat16), 'wid').astype(jnp.float32)  43.1 us
    pmax x1, blocking collectives, body(): peak = lax.pmax(local_peak, ('grp', 'ctx'))  39 us
    psum x1, blocking collectives, body(): weight_sum, weighted = lax.psum((weight_sum, weighted), ('grp', 'ctx'))  34.2 us
    all_gather x1, blocking collectives, body(): error_all = lax.all_gather(scaled_error, ('grp', 'ctx'), axis=0, tiled=True)  32.2 us
    all_gather x1, blocking collectives, body(): lax.all_gather(layer_out, ('grp', 'ctx'))  31.8 us
    psum x1, waiting for transfers between devices, body(): lax.psum(latent_part.astype(jnp.bfloat16), 'wid').astype(jnp.float32)  30.7 us
  transfers between devices with their start and end apart: 5, of which 5 were waited for; matrix products, arithmetic and copies ran while one was open for 2% of the time, Pallas kernels for 0%

profile of v1, /device:TPU:0, one launch (start us, length us, event | category | flops | bytes accessed | tf_op | source)
XLA Modules:
  0.0 458.8 jit_solution(13159831020779658017)
XLA Ops:
  7.2 0.0 copy-start
  7.2 0.0 all-reduce.4.cloned.1.call-start
  7.2 0.9 le.20
  8.1 0.8 select_reduce_fusion.1
  9.0 0.1 iota_add_fusion
  9.0 0.1 iota_compare_fusion
  9.1 0.1 compare_and_fusion
  9.3 3.8 fusion.2
  13.0 39.0 %pmax.7 = f32[4,64,2,8]{1,3,2,0:T(8,128)S(1)} all-reduce(f32[4,64,2,8]{1,3,2,0:T(8,128)S(1)} %get-tuple-element.11), channel_id=1, replica_groups=mesh['grp'=4,'ctx'=2,'wid'=4] {'grp','ctx'}, use_global_device_ids=true, to_apply=%region_3.4 | all-reduce | flops 4096 | bytes 32768 | tf_op jit(solution)/shard_map/pmax | solution.py:42
  52.0 3.2 fusion.5
  55.3 2.4 copy.29
  57.7 3.0 convolution_bitcast_fusion
  60.6 0.0 all-reduce.4.cloned.1.call-update
  60.7 0.0 reduce-scatter.3.cloned.1.call-start
  60.7 34.2 %psum.29 = f32[4,64,2,8]{1,3,2,0:T(8,128)S(1)} all-reduce(f32[4,64,2,8]{1,3,2,0:T(8,128)S(1)} %get-tuple-element.9), channel_id=1, replica_groups=mesh['grp'=4,'ctx'=2,'wid'=4] {'grp','ctx'}, use_global_device_ids=true, to_apply=%region_6.7 | all-reduce | flops 4096 | bytes 32768 | tf_op jit(solution)/shard_map/psum | solution.py:50
  94.9 0.1 copy.31
  95.0 65.7 %all-reduce.4.cloned.1.call-done = f32[4,64,2,8,128]{4,3,1,2,0:T(8,128)} async-done(((f32[4,64,2,8,128]{4,3,1,2,0:T(8,128)}), f32[4,64,2,8,128]{4,3,1,2,0:T(8,128)}) %all-reduce.4.cloned.1.call-update) | async-done | bytes 2097168 | tf_op jit(solution)/shard_map/psum | solution.py:50
  160.8 1.9 divide_convert_fusion
  162.7 1.2 copy.32
  163.9 2.3 reshape.76
  166.2 2.9 convolution_convert_fusion.4
  169.1 0.0 reduce-scatter.3.cloned.1.call-update
  169.1 0.0 all-reduce.6.cloned.1.call-start
  169.2 19.8 %reduce-scatter.3.cloned.1.call-done = bf16[64,640]{1,0:T(8,128)(2,1)} async-done(((bf16[256,640]{1,0:T(8,128)(2,1)}), bf16[64,640]{1,0:T(8,128)(2,1)}) %reduce-scatter.3.cloned.1.call-update) | async-done | bytes 81936 | tf_op jit(solution)/shard_map/reduce_scatter | solution.py:54
  189.0 0.9 add_convert_fusion
  189.9 31.8 %all-gather = bf16[512,640]{1,0:T(8,128)(2,1)S(1)} all-gather(bf16[64,640]{1,0:T(8,128)(2,1)S(1)} %add_convert_fusion), channel_id=2, replica_groups=mesh['grp'=4,'ctx'=2,'wid'=4] {'grp','ctx'}, dimensions={0}, use_global_device_ids=true | all-gather | bytes 737280 | tf_op jit(solution)/shard_map/all_gather | solution.py:58
  221.7 0.4 copy.52
  222.1 1.3 all_to_all.14
  223.3 1.2 copy.34
  224.5 12.6 %all_to_all.19 = bf16[64,4,1280]{2,0,1:T(8,128)(2,1)S(1)} all-to-all(bf16[64,4,1280]{2,0,1:T(8,128)(2,1)S(1)} %copy.34), channel_id=1, replica_groups=mesh['grp'=4,'ctx'=2,'wid'=4] {'wid'}, dimensions={1} | all-to-all | bytes 1310720 | tf_op jit(solution)/shard_map/all_to_all | solution.py:59
  237.1 6.6 %convolution_convert_fusion.3 = bf16[256,3072]{1,0:T(8,128)(2,1)} fusion(bf16[256,1280]{1,0:T(8,128)(2,1)S(1)} %bitcast.38, bf16[1280,3072]{1,0:T(8,128)(2,1)} %param.18), kind=kOutput, calls=%fused_computation.4 | convolution fusion | flops 2014052352 | bytes 10092544 | tf_op jit(solution)/shard_map/dot_general | solution.py:60
  243.7 0.0 all-reduce.6.cloned.1.call-update
  243.7 0.0 reduce-scatter.5.cloned.1.call-start
  243.8 43.1 %all-reduce.6.cloned.1.call-done = bf16[256,3072]{1,0:T(8,128)(2,1)} async-done(((bf16[256,3072]{1,0:T(8,128)(2,1)}), bf16[256,3072]{1,0:T(8,128)(2,1)}) %all-reduce.6.cloned.1.call-update) | async-done | bytes 1572880 | tf_op jit(solution)/shard_map/psum | solution.py:61
  286.9 8.8 %fusion.12 = f32[256,1280]{1,0:T(8,128)} fusion(bf16[3072,1280]{1,0:T(8,128)(2,1)} %param.20, bf16[256,3072]{1,0:T(8,128)(2,1)} %all-reduce.6.cloned.1.call-done, f32[3072]{0:T(1024)S(1)} %copy-done.5), kind=kOutput, calls=%fused_computation.35 | convolution fusion | flops 2021916672 | bytes 10760192 | tf_op jit(solution)/shard_map/dot_general | solution.py:65
  295.7 0.0 reduce-scatter.5.cloned.1.call-update
  295.7 0.0 all-reduce.8.cloned.1.call-start
  295.8 65.3 %reduce-scatter.5.cloned.1.call-done = f32[32,1280]{1,0:T(8,128)} async-done(((f32[256,1280]{1,0:T(8,128)}), f32[32,1280]{1,0:T(8,128)}) %reduce-scatter.5.cloned.1.call-update) | async-done | bytes 163856 | tf_op jit(solution)/shard_map/reduce_scatter | solution.py:64
  361.1 0.9 multiply_convert_fusion.1
  362.0 32.2 %all_gather.11 = bf16[256,1280]{1,0:T(8,128)(2,1)S(1)} all-gather(bf16[32,1280]{1,0:T(8,128)(2,1)S(1)} %multiply_convert_fusion.1), channel_id=1, replica_groups=mesh['grp'=4,'ctx'=2,'wid'=4] {'grp','ctx'}, dimensions={0}, use_global_device_ids=true | all-gather | bytes 737280 | tf_op jit(solution)/shard_map/all_gather | solution.py:75
  394.2 0.8 copy-done.1
  395.0 6.6 %convolution_convert_fusion.2 = bf16[256,3072]{1,0:T(8,128)(2,1)} fusion(bf16[256,1280]{1,0:T(8,128)(2,1)S(1)} %all_gather.11, bf16[3072,1280]{1,0:T(8,128)(2,1)} %param.20), kind=kOutput, calls=%fused_computation.3 | convolution fusion | flops 2014052352 | bytes 10092544 | tf_op jit(solution)/shard_map/dot_general | solution.py:77
  401.6 0.0 all-reduce.8.cloned.1.call-update
  401.7 1.8 convert_reduce_fusion.1
  403.4 9.0 %convolution_convert_fusion = bf16[3072,1280]{1,0:T(8,128)(2,1)} fusion(bf16[256,1280]{1,0:T(8,128)(2,1)} %copy-done.1, bf16[256,3072]{1,0:T(8,128)(2,1)} %all-reduce.6.cloned.1.call-done, f32[3072]{0:T(1024)S(1)} %copy-done.5), kind=kOutput, calls=%fused_computation | convolution fusion | flops 2025848832 | bytes 10104832 | tf_op jit(solution)/shard_map/dot_general | solution.py:80
  412.5 30.7 %all-reduce.8.cloned.1.call-done = bf16[256,3072]{1,0:T(8,128)(2,1)} async-done(((bf16[256,3072]{1,0:T(8,128)(2,1)}), bf16[256,3072]{1,0:T(8,128)(2,1)}) %all-reduce.8.cloned.1.call-update) | async-done | bytes 1572880 | tf_op jit(solution)/shard_map/psum | solution.py:83
  443.2 3.6 convert_reduce_fusion
  446.8 5.5 %convolution_convert_fusion.1 = bf16[1280,3072]{1,0:T(8,128)(2,1)} fusion(bf16[256,1280]{1,0:T(8,128)(2,1)S(1)} %bitcast.40, bf16[256,3072]{1,0:T(8,128)(2,1)S(1)} %get-tuple-element.8), kind=kOutput, calls=%fused_computation.1 | convolution fusion | flops 2017198080 | bytes 10092544 | tf_op jit(solution)/shard_map/dot_general | solution.py:85
  (13 shorter events, 0.0 us)
Async XLA Ops:
  7.2 159.0 %copy-start = (bf16[2048,640]{1,0:T(8,128)(2,1)S(1)}, bf16[2048,640]{1,0:T(8,128)(2,1)}, u32[]{:S(2)}) copy-start(bf16[2048,640]{1,0:T(8,128)(2,1)} %param.17) | copy-start | bytes 7864324
  7.2 153.6 %all-reduce.4.cloned.1.call-start = ((), (), s32[]{:S(2)}) async-start(), calls=%async_computation.3 | async-start | bytes 4194304 | tf_op jit(solution)/shard_map/psum | solution.py:50
  13.0 44.6 %copy-start.3 = (bf16[4,64,2,128]{3,2,1,0:T(2,128)(2,1)S(1)}, bf16[4,64,2,128]{3,2,1,0:T(2,128)(2,1)}, u32[]{:S(2)}) copy-start(bf16[4,64,2,128]{3,2,1,0:T(2,128)(2,1)} %param.13) | copy-start | bytes 393220
  60.7 128.4 %reduce-scatter.3.cloned.1.call-start = ((), (), s32[]{:S(2)}) async-start(), calls=%async_computation.4 | async-start | bytes 409600 | tf_op jit(solution)/shard_map/reduce_scatter | solution.py:54
  163.9 25.1 %copy-start.4 = (bf16[64,640]{1,0:T(8,128)(2,1)S(1)}, bf16[64,640]{1,0:T(8,128)(2,1)}, u32[]{:S(2)}) copy-start(bf16[64,640]{1,0:T(8,128)(2,1)} %param.16) | copy-start | bytes 245764
  169.1 117.7 %all-reduce.6.cloned.1.call-start = ((), (), s32[]{:S(2)}) async-start(), calls=%async_computation.5 | async-start | bytes 3145728 | tf_op jit(solution)/shard_map/psum | solution.py:61
  189.9 53.8 %copy-start.2 = (bf16[64,640]{1,0:T(8,128)(2,1)}, bf16[64,640]{1,0:T(8,128)(2,1)S(1)}, u32[]{:S(2)}) copy-start(bf16[64,640]{1,0:T(8,128)(2,1)S(1)} %add_convert_fusion) | copy-start | bytes 245764
  237.1 49.7 %copy-start.5 = (f32[3072]{0:T(1024)S(1)}, f32[3072]{0:T(1024)}, u32[]{:S(2)}) copy-start(f32[3072]{0:T(1024)} %param.19) | copy-start | bytes 36868
  243.7 117.3 %copy-start.6 = (f32[1280]{0:T(1024)S(1)}, f32[1280]{0:T(1024)}, u32[]{:S(2)}) copy-start(f32[1280]{0:T(1024)} %param.21) | copy-start | bytes 15364
  243.7 117.3 %reduce-scatter.5.cloned.1.call-start = ((), (), s32[]{:S(2)}) async-start(), calls=%async_computation.6 | async-start | bytes 1474560 | tf_op jit(solution)/shard_map/reduce_scatter | solution.py:64
  295.7 147.5 %all-reduce.8.cloned.1.call-start = ((), (), s32[]{:S(2)}) async-start(), calls=%async_computation.7 | async-start | bytes 3145728 | tf_op jit(solution)/shard_map/psum | solution.py:83
  394.2 0.8 copy-start.1
Sparse Core Ops, SparseCore 0:
  60.8 99.9 all-reduce.3
  169.3 19.6 reduce-scatter.2
  243.8 42.9 all-reduce.5
  295.8 65.1 reduce-scatter.4
  401.8 41.3 all-reduce.7
